TPU v7x, 256 devices: a whole 4x4x8 slice. The times are simulated.
256 devices in a mesh: date: 16 (over z, core), pix: 16 (over y, x).
Axes of the slice: x: 4, y: 4, z: 8, core: 2. Of those that a mesh axis runs over, the one named last changes fastest.
Arguments:
- bin_index: int32 [256, 1048576], P('date', 'pix'), may hold values from 0 to 511
- clear_mask: bfloat16 [256, 1048576], P('date', 'pix'), may hold values from 0 to 1, as said below
Outputs:
- anomaly: float32 [3, 8192], P(None, 'pix')
- tile_levels: float32 [3], replicated
Inputs may be any that keep to these rules, and one draw needn't show every extreme that they name: `clear_mask`: 0 for a cloudy observation, else a positive weight.
All inputs are finite; a program needn't handle non-finite values.
Results may differ from a plain program's by a relative error of at most 0.0003.
Values sent between devices are 32-bit elements; how exact they have to be, the bound alone decides.
A program may use at most 64 MiB of HBM per device.

v0:
```python
import functools

import jax
import jax.numpy as jnp
from jax import lax
from jax.sharding import Mesh
from jax.sharding import PartitionSpec as P

BINS = 512
BLOCK = 128
DATE = ("date_0", "date_1")
DATE_PIX = ("date_0", "date_1", "pix_0", "pix_1")
PIX = ("pix_0", "pix_1")


QUANTILES = (0.1, 0.5, 0.9)
LOW_EDGE = -1.0


def cut_along(x, dim, devices):
    lengths = x.shape
    blocks = x.reshape(*lengths[:dim], devices, lengths[dim] // devices, *lengths[dim + 1 :])
    return jnp.moveaxis(blocks, dim, 0)


def summed_on_arrival(x, axis, dim):
    blocks = cut_along(x, dim, lax.axis_size(axis))
    arrived = lax.all_to_all(blocks, axis, split_axis=0, concat_axis=0, tiled=True)
    return arrived.sum(axis=0)


def over_axes(x, axes):
    return functools.reduce(lax.psum, axes, x)


def from_everyone(x, axis):
    copies = jnp.broadcast_to(x, (lax.axis_size(axis), *x.shape))
    return lax.all_to_all(copies, axis, split_axis=0, concat_axis=0, tiled=True)


def laid_out(blocks, dim):
    lengths = list(blocks.shape[1:])
    lengths[dim] *= blocks.shape[0]
    return jnp.moveaxis(blocks, 0, dim).reshape(lengths)


def gathered_copies(x, axis, dim):
    blocks = from_everyone(x, axis)
    return laid_out(blocks, dim)


def percentiles(counts, before, totals):
    target = jnp.stack([quantile * totals + 0.25 for quantile in QUANTILES])
    passed = jnp.clip(
        (target[:, :, None] - before[None]) / jnp.maximum(counts, 1.0)[None], 0.0, 1.0
    )
    return LOW_EDGE + 2.0 / BINS * jnp.sum(passed, axis=2)


def block_counts(bin_index, clear_mask, blocks):
    chosen = bin_index
    frames = chosen.shape[0]
    chosen = jnp.moveaxis(chosen.reshape(frames, blocks, BLOCK), 1, 0)
    weight = jnp.moveaxis(clear_mask.reshape(frames, blocks, BLOCK), 1, 0)
    upper_digit = chosen // 16
    lower_digit = chosen % 16
    upper_values = jnp.arange(BINS // 16, dtype=jnp.int32)
    lower_values = jnp.arange(16, dtype=jnp.int32)
    upper_table = jnp.where(
        upper_digit[:, None] == upper_values[None, :, None, None],
        weight[:, None],
        jnp.zeros((), jnp.bfloat16),
    )
    lower_table = (lower_digit[:, None] == lower_values[None, :, None, None]).astype(jnp.bfloat16)
    joint_counts = jnp.einsum(
        "ghdp,gldp->ghl", upper_table, lower_table, preferred_element_type=jnp.float32
    )
    return joint_counts.reshape(blocks, BINS)


def body(bin_index, clear_mask):
    date_devices = lax.axis_size(DATE)
    blocks_here = bin_index.shape[1] // BLOCK
    owned_rows = blocks_here // date_devices
    triangle = (jnp.arange(BINS)[:, None] < jnp.arange(BINS)[None, :]).astype(jnp.float32)
    owned_sums = summed_on_arrival(
        block_counts(bin_index, clear_mask, owned_rows * lax.axis_size(DATE)), DATE, 0
    )
    tile_counts = over_axes(jnp.sum(owned_sums, axis=0), DATE_PIX)
    tile_before = jnp.cumsum(tile_counts) - tile_counts
    tile_levels = percentiles(tile_counts[None], tile_before[None], jnp.sum(tile_counts)[None])[
        :, 0
    ]
    before = jnp.dot(owned_sums, triangle, precision=lax.Precision.HIGHEST)
    owned_levels = (
        percentiles(owned_sums, before, jnp.sum(owned_sums, axis=1)) - tile_levels[:, None]
    )
    anomaly = gathered_copies(owned_levels, DATE, 1)
    return (anomaly, tile_levels)


def solution(mesh):
    torus = Mesh(mesh.devices.reshape(8, 2, 4, 4), ("date_0", "date_1", "pix_0", "pix_1"))
    in_specs = (P(DATE, PIX), P(DATE, PIX))
    out_specs = (P(None, PIX), P())
    return jax.shard_map(body, mesh=torus, in_specs=in_specs, out_specs=out_specs, check_vma=False)
```

profile of v0, /device:TPU:1, one launch (start us, length us, event | category | flops | bytes accessed | tf_op | source)
XLA Modules:
  0.0 136.4 jit_solution(10786459747797640972)
XLA Ops:
  0.6 3.0 %copy.44 = s32[2,8,512,128]{3,2,1,0:T(8,128)S(1)} copy(s32[2,8,512,128]{3,1,2,0:T(8,128)} %bitcast.77) | data formatting | bytes 8388608
  3.6 3.8 %add_select_fusion.1 = (s32[512,16,128]{2,0,1:T(8,128)S(1)}, s32[512,16,128]{2,0,1:T(8,128)S(1)}) fusion(s32[2,8,512,128]{3,2,1,0:T(8,128)S(1)} %copy.44), kind=kLoop, calls=%fused_computation.9 | loop fusion | flops 19922944 | bytes 12582912 | tf_op jit(solution)/shard_map/jit(floor_divide)/jit(_where)/select_n | solution.py:65
  7.5 2.4 %copy.34 = s32[512,16,128]{2,1,0:T(8,128)S(1)} copy(s32[512,16,128]{2,0,1:T(8,128)S(1)} %get-tuple-element.5) | data formatting | bytes 8388608 | tf_op jit(solution)/shard_map/jit(floor_divide)/jit(_where)/select_n | solution.py:65
  9.9 0.0 copy-start
  9.9 2.4 %copy.36 = s32[512,16,128]{2,1,0:T(8,128)S(1)} copy(s32[512,16,128]{2,0,1:T(8,128)S(1)} %get-tuple-element.6) | data formatting | bytes 8388608 | tf_op jit(solution)/shard_map/jit(remainder)/select_n | solution.py:66
  12.4 0.0 copy-done
  12.4 0.4 copy.45
  12.8 1.4 copy.35
  14.1 20.1 %fusion.10 = f32[512,32,16]{1,2,0:T(8,128)} fusion(s32[512,16,128]{2,1,0:T(8,128)S(1)} %copy.36, s32[512,16,128]{2,1,0:T(8,128)S(1)} %copy.34, bf16[512,16,128]{2,1,0:T(8,128)(2,1)S(1)} %copy.35), kind=kOutput, calls=%fused_computation.18 | convolution fusion | flops 1157627904 | bytes 11534336 | tf_op jit(solution)/shard_map/ghdp,gldp->ghl/dot_general | solution.py:75
  34.2 3.2 %copy.37 = f32[512,32,16]{0,2,1:T(8,128)S(1)} copy(f32[512,32,16]{1,2,0:T(8,128)} %fusion.10) | data formatting | bytes 2097152 | tf_op jit(solution)/shard_map/ghdp,gldp->ghl/dot_general | solution.py:75
  37.5 2.5 %reshape_reshape.3 = f32[16,32,512]{1,0,2:T(8,128)} reshape(f32[512,32,16]{0,2,1:T(8,128)S(1)} %copy.37) | data formatting | bytes 2097152 | tf_op jit(solution)/shard_map/reshape;reshape | solution.py:22
  40.0 2.8 %copy.38 = f32[16,32,512]{2,1,0:T(8,128)S(1)} copy(f32[16,32,512]{1,0,2:T(8,128)} %reshape_reshape.3) | data formatting | bytes 2097152 | tf_op jit(solution)/shard_map/reshape;reshape | solution.py:22
  42.8 38.2 %all_to_all.10 = f32[16,32,512]{2,1,0:T(8,128)S(1)} all-to-all(f32[16,32,512]{2,1,0:T(8,128)S(1)} %copy.38), channel_id=1, replica_groups=mesh['date_0'=8,'date_1'=2,'pix_0'=4,'pix_1'=4] {'date_0','date_1'}, dimensions={0} | all-to-all | bytes 2097152 | tf_op jit(solution)/shard_map/all_to_all | solution.py:28
  81.0 0.2 fusion.15
  81.2 0.3 fusion.13
  81.5 11.0 %psum.28 = f32[512]{0:T(512)S(1)} all-reduce(f32[512]{0:T(512)S(1)} %get-tuple-element.2), channel_id=1, replica_groups=mesh['date_0'=8,'date_1'=2,'pix_0'=4,'pix_1'=4] {'date_0'}, use_global_device_ids=true, to_apply=%region_4.5 | all-reduce | flops 512 | bytes 4096 | tf_op jit(solution)/shard_map/psum | solution.py:33
  92.5 4.9 %psum.29 = f32[512]{0:T(512)S(1)} all-reduce(f32[512]{0:T(512)S(1)} %psum.28), channel_id=1, replica_groups=mesh['date_0'=8,'date_1'=2,'pix_0'=4,'pix_1'=4] {'date_1'}, use_global_device_ids=true, to_apply=%region_5.6 | all-reduce | flops 512 | bytes 4096 | tf_op jit(solution)/shard_map/psum | solution.py:33
  97.4 8.7 %psum.30 = f32[512]{0:T(512)S(1)} all-reduce(f32[512]{0:T(512)S(1)} %psum.29), channel_id=1, replica_groups=mesh['date_0'=8,'date_1'=2,'pix_0'=4,'pix_1'=4] {'pix_0'}, use_global_device_ids=true, to_apply=%region_6.7 | all-reduce | flops 512 | bytes 4096 | tf_op jit(solution)/shard_map/psum | solution.py:33
  106.1 8.5 %psum.31 = f32[512]{0:T(512)S(1)} all-reduce(f32[512]{0:T(512)S(1)} %psum.30), channel_id=1, replica_groups=mesh['date_0'=8,'date_1'=2,'pix_0'=4,'pix_1'=4] {'pix_1'}, use_global_device_ids=true, to_apply=%region_7.8 | all-reduce | flops 512 | bytes 4096 | tf_op jit(solution)/shard_map/psum | solution.py:33
  114.5 0.3 reduce-window.9
  114.8 0.1 slice.7
  114.9 0.1 slice_reduce_fusion
  115.1 0.6 fusion.16
  117.6 0.1 maximum_bitcast_fusion
  117.7 0.2 clamp_reduce_fusion.1
  117.9 0.0 copy-start.1
  117.9 0.2 clamp_reduce_fusion
  118.1 0.1 add_subtract_fusion
  118.2 17.5 %all_to_all.11 = f32[16,3,32]{2,1,0:T(4,128)S(1)} all-to-all(f32[16,3,32]{2,1,0:T(4,128)S(1)} %broadcast_in_dim.16), channel_id=1, replica_groups=mesh['date_0'=8,'date_1'=2,'pix_0'=4,'pix_1'=4] {'date_0','date_1'}, dimensions={0} | all-to-all | bytes 12288 | tf_op jit(solution)/shard_map/all_to_all | solution.py:38
  135.7 0.7 reshape.186
  136.4 0.0 copy-done.1
  (7 shorter events, 0.1 us)
Async XLA Ops:
  9.9 2.5 %copy-start = (bf16[16,65536]{1,0:T(8,128)(2,1)S(1)}, bf16[16,65536]{1,0:T(8,128)(2,1)}, u32[]{:S(2)}) copy-start(bf16[16,65536]{1,0:T(8,128)(2,1)} %param.3) | copy-start | bytes 6291460
  117.9 18.5 %copy-start.1 = (f32[3]{0:T(128)}, f32[3]{0:T(128)S(1)}, u32[]{:S(2)}) copy-start(f32[3]{0:T(128)S(1)} %multiply_add_fusion) | copy-start | bytes 40
where the time goes:
time: 137 us; the launch traced here: 136 us
  blocking collectives  88.7 us (65%)
  matrix products  20.4 us (15%)
  local copies, waits for them, and re-layouts  19 us (14%)
  other arithmetic  5.54 us (4%)
  between operations  2.68 us (2%)
    all_to_all x1, blocking collectives, summed_on_arrival(): lax.all_to_all(blocks, axis, split_axis=0, concat_axis=0, tiled=True)  38.2 us
    psum x4, blocking collectives, over_axes(): return functools.reduce(lax.psum, axes, x)  33 us
    dot_general x1, matrix products, block_counts(): jnp.einsum('ghdp,gldp->ghl', upper_table, lower_table, preferred_element_...  20.1 us
    all_to_all x1, blocking collectives, from_everyone(): return lax.all_to_all(copies, axis, split_axis=0, concat_axis=0, tiled=True)  17.5 us
    another operation x2, local copies, waits for them, and re-layouts, cut_along(): x.reshape(*lengths[:dim], devices, lengths[dim] // devices, *lengths[dim...  5.29 us
    select_n x1, other arithmetic, block_counts(): upper_digit = chosen // 16  3.84 us
    unnamed x6, local copies, waits for them, and re-layouts  3.39 us
    dot_general x1, local copies, waits for them, and re-layouts, block_counts(): jnp.einsum('ghdp,gldp->ghl', upper_table, lower_table, preferred_element_...  3.23 us

commit v1 on v0

v1 whole, which is shorter than its diff:
```python
import functools

import jax
import jax.numpy as jnp
from jax import lax
from jax.experimental import pallas as pl
from jax.experimental.pallas import tpu as pltpu
from jax.sharding import PartitionSpec as P

BINS = 512
BLOCK = 128
UPPER = 16
LOWER = 32
JOINED = 8
QUANTILES = (0.1, 0.5, 0.9)
LOW_EDGE = -1.0
MESH = pl.DeviceIdType.MESH
bf16 = jnp.bfloat16
f32 = jnp.float32
f8 = jnp.float8_e4m3fn


def iota(shape, dim):
    return lax.broadcasted_iota(jnp.int32, shape, dim)


def ones_where(mask):
    return jnp.where(mask, 1.0, 0.0).astype(bf16)


def pieces(x):
    first = x.astype(bf16)
    rest = x - first.astype(f32)
    second = rest.astype(bf16)
    third = (rest - second.astype(f32)).astype(bf16)
    return first, second, third


def count_group(idx_ref, w_ref, base, acc, mxu):
    upper_rows = (iota((UPPER, 128), 0) * LOWER).astype(jnp.int16)
    lower_rows = iota((LOWER, 128), 0).astype(jnp.int16)
    lefts, rights = [], []
    frames = idx_ref.shape[0]
    for j in range(JOINED):
        lanes = pl.ds(pl.multiple_of(base + 128 * j, 128), 128)
        bins = idx_ref[:, lanes].astype(jnp.int16)
        weight = w_ref[:, lanes]
        upper = bins & jnp.int16((UPPER - 1) * LOWER)
        lower = bins & jnp.int16(LOWER - 1)
        left, right = [], []
        for f in range(frames):
            row = slice(f, f + 1)
            is_upper = jnp.broadcast_to(upper[row], (UPPER, 128)) == upper_rows
            is_lower = jnp.broadcast_to(lower[row], (LOWER, 128)) == lower_rows
            left.append(jnp.where(is_upper, jnp.broadcast_to(weight[row], (UPPER, 128)), jnp.zeros((), bf16)))
            right.append(jnp.where(is_lower, jnp.ones((), f8), jnp.zeros((), f8)))
        lefts.append(left)
        rights.append(right)
    for k in range(frames // 2):
        pair = (2 * k, 2 * k + 1)
        left = jnp.concatenate([jnp.concatenate([x[f] for f in pair], axis=1) for x in lefts], axis=0)
        right = jnp.concatenate([jnp.concatenate([x[f] for f in pair], axis=1) for x in rights], axis=0)
        pltpu.matmul_push_rhs(right, staging_register=k % 2, mxu_index=mxu, transpose=True)
        pltpu.matmul_acc_lhs(acc, left, load_staged_rhs=k % 2)
    joint = pltpu.matmul_pop(acc)
    lane = iota((UPPER, 128), 1)
    halves = []
    for half in range(2):
        own = None
        for q in range(4):
            j = 4 * half + q
            part = joint[j * UPPER : (j + 1) * UPPER, half * 128 : (half + 1) * 128]
            own = part if own is None else jnp.where(lane >= q * LOWER, part, own)
        halves.append(own)
    return jnp.concatenate(halves, axis=1)


def triple_matmul(acc, x, register):
    for n, piece in enumerate(pieces(x)):
        pltpu.matmul_acc_lhs(acc, piece, load_staged_rhs=register if n == 0 else None)


def block_levels(counts, acc_prefix, acc_rows, acc_below, acc_sums):
    flat = counts.reshape(64, 256)
    r, c = iota((256, 256), 0), iota((256, 256), 1)
    same = (r // LOWER) == (c // LOWER)
    pltpu.matmul_push_rhs(ones_where(same & (r % LOWER < c % LOWER)), staging_register=0, mxu_index=0)
    pltpu.matmul_push_rhs(ones_where(same), staging_register=0, mxu_index=1)
    triple_matmul(acc_prefix, flat, 0)
    triple_matmul(acc_rows, flat, 0)
    row_sums = pltpu.matmul_pop(acc_rows)
    stacked = jnp.concatenate([*pieces(row_sums), jnp.zeros((64, 256), bf16)], axis=0)
    pltpu.matmul_push_rhs(stacked, staging_register=0, mxu_index=0)
    i, k = iota((128, 256), 0), iota((128, 256), 1)
    chosen = ((i % 64) // UPPER == (k % 64) // UPPER) & (k < 192) & ((k % UPPER < i % UPPER) | (i >= 64))
    pltpu.matmul_acc_lhs(acc_below, ones_where(chosen), load_staged_rhs=0)
    within = pltpu.matmul_pop(acc_prefix)
    below = pltpu.matmul_pop(acc_below)
    before = within + below[:64]
    total = below[64:]
    floor = jnp.maximum(flat, 1.0)
    passed = [jnp.clip((q * total + 0.25 - before) / floor, 0.0, 1.0) for q in QUANTILES]
    for g in range(4):
        pltpu.matmul_push_rhs(
            ones_where((c % LOWER) == JOINED * g + r // LOWER), staging_register=0, mxu_index=1
        )
        rows = jnp.concatenate([p[g * UPPER : (g + 1) * UPPER] for p in passed], axis=0)
        triple_matmul(acc_sums, rows, 0)
    sums = pltpu.matmul_pop(acc_sums)[:, :128]
    row = iota((8, 128), 0)
    out = jnp.zeros((8, 128), f32)
    for q in range(3):
        value = jnp.sum(sums[q * UPPER : (q + 1) * UPPER], axis=0, keepdims=True)
        out = jnp.where(row == q, LOW_EDGE + 2.0 / BINS * value, out)
    return out


def push_tile_tables(register):
    r, c = iota((256, 256), 0), iota((256, 256), 1)
    same = (r % 128) // 64 == (c % 128) // 64
    counts = same & (r % LOWER == c % LOWER) & (c < 128)
    prefix = same & (r % LOWER < c % LOWER) & (c >= 128)
    pltpu.matmul_push_rhs(ones_where(counts | prefix), staging_register=register, mxu_index=0)
    pltpu.matmul_push_rhs(ones_where(same | (c >= 128)), staging_register=register, mxu_index=1)


def tile_of(total, acc_a, acc_b, register):
    p1, p2, p3 = pieces(total)
    zero = jnp.zeros((8, 128), f32)
    left = jnp.concatenate(
        [
            jnp.concatenate([p1.astype(f32), p3.astype(f32)], axis=0),
            jnp.concatenate([p2.astype(f32), zero], axis=0),
        ],
        axis=1,
    ).astype(bf16)
    pltpu.matmul_acc_lhs(acc_a, left, load_staged_rhs=register)
    pltpu.matmul_acc_lhs(acc_b, left, load_staged_rhs=register)
    a = pltpu.matmul_pop(acc_a)
    b = pltpu.matmul_pop(acc_b)
    a = a[:8] + a[8:]
    b = b[:8] + b[8:]
    counts, within = a[:, :128], a[:, 128:]
    same_rows, all_rows = b[:, :128], b[:, 128:]
    row, lane = iota((8, 128), 0), iota((8, 128), 1)
    below = jnp.where(row >= 1, pltpu.roll(same_rows, 1, 0), 0.0)
    for shift in (1, 2, 4):
        below = below + jnp.where(row >= shift, pltpu.roll(below, shift, 0), 0.0)
        same_rows = same_rows + pltpu.roll(same_rows, shift, 0)
        all_rows = all_rows + pltpu.roll(all_rows, shift, 0)
    before = within + below + jnp.where(lane >= 64, all_rows - same_rows, 0.0)
    floor = jnp.maximum(counts, 1.0)
    levels = []
    for q in QUANTILES:
        passed = jnp.clip((q * all_rows + 0.25 - before) / floor, 0.0, 1.0)
        both = jnp.sum(jnp.sum(passed, axis=0, keepdims=True), axis=1, keepdims=True)
        levels.append(LOW_EDGE + 2.0 / BINS * (0.5 * both))
    return levels


def kernel(
    dates,
    pixs,
    idx_hbm,
    w_hbm,
    anomaly_ref,
    tile_ref,
    idx_v,
    w_v,
    raw,
    part_out,
    part_in,
    own,
    ici_in,
    tile_acc,
    pix_in,
    date_in,
    level_in,
    in_sem,
    core_send,
    core_recv,
    ici_send,
    ici_recv,
    pix_send,
    pix_recv,
    date_send,
    date_recv,
    level_send,
    level_recv,
):
    d = lax.axis_index("date")
    p = lax.axis_index("pix")
    z = lax.div(d, 2)
    core = lax.rem(d, 2)
    rings = dates // 2
    owner_lanes = idx_v.shape[1] // dates
    chunk = 2 * owner_lanes
    half = rings // 2

    def offset_of(s):
        odd = lax.rem(s, 2)
        return half + (1 - odd) * lax.div(s, 2) - odd * lax.div(s + 1, 2)

    def ring_at(s):
        return lax.rem(z + offset_of(s), rings)

    def load(s):
        lanes = pl.ds(pl.multiple_of(ring_at(s) * chunk, 128), chunk)
        return (
            pltpu.make_async_copy(idx_hbm.at[:, lanes], idx_v.at[:, lanes], in_sem.at[0, s]),
            pltpu.make_async_copy(w_hbm.at[:, lanes], w_v.at[:, lanes], in_sem.at[1, s]),
        )

    for s in range(rings):
        for copy in load(s):
            copy.start()

    barrier = pltpu.get_barrier_semaphore()
    for k in range(1, dates):
        pl.semaphore_signal(barrier, inc=1, device_id={"date": lax.rem(d + k, dates)}, device_id_type=MESH)
    for k in range(1, pixs):
        pl.semaphore_signal(barrier, inc=1, device_id={"pix": lax.rem(p + k, pixs)}, device_id_type=MESH)

    def to_core(s):
        return pltpu.make_async_remote_copy(
            src_ref=part_out.at[s],
            dst_ref=part_in.at[s],
            send_sem=core_send.at[s],
            recv_sem=core_recv.at[s],
            device_id={"date": d + 1 - 2 * core},
            device_id_type=MESH,
        )

    def to_ring(s):
        off = offset_of(s)
        return pltpu.make_async_remote_copy(
            src_ref=own.at[s],
            dst_ref=ici_in.at[off],
            send_sem=ici_send.at[s],
            recv_sem=ici_recv.at[off],
            device_id={"date": 2 * lax.rem(z + off, rings) + core},
            device_id_type=MESH,
        )

    def to_all(buffer, axis, me, size, k, send, recv):
        return pltpu.make_async_remote_copy(
            src_ref=buffer.at[me],
            dst_ref=buffer.at[me],
            send_sem=send.at[k],
            recv_sem=recv.at[me],
            device_id={axis: lax.rem(me + k, size)},
            device_id_type=MESH,
        )

    def from_all(buffer, axis, me, size, k, send, recv):
        source = lax.rem(me + k, size)
        return pltpu.make_async_remote_copy(
            src_ref=buffer.at[source],
            dst_ref=buffer.at[source],
            send_sem=send.at[k],
            recv_sem=recv.at[source],
            device_id={axis: source},
            device_id_type=MESH,
        )

    to_pix = (pix_in, "pix", p, pixs)
    to_date = (date_in, "date", d, dates)
    to_level = (level_in, "date", d, dates)

    def body(acc_a, acc_b, acc_c, acc_d, acc_prefix, acc_rows, acc_sums, acc_ta, acc_tb):
        tile_acc[...] = jnp.zeros_like(tile_acc)

        def step(s, carry):
            for copy in load(s):
                copy.wait()
            ring = ring_at(s)
            sums = None
            for m in range(8):
                side = 1 - core if m < 4 else core
                base = (2 * ring + side) * owner_lanes + (m % 4) * (JOINED * BLOCK)
                counts = count_group(idx_v, w_v, base, (acc_a, acc_b, acc_c, acc_d)[m % 4], m % 2)
                if m < 4:
                    part_out[s, m] = counts
                else:
                    raw[s, m - 4] = counts
                sums = counts if sums is None else sums + counts
            tile_acc[...] += sums

            @pl.when(s == 0)
            def _():
                pl.semaphore_wait(barrier, dates + pixs - 2)

            @pl.when(s >= 1)
            def _():
                to_core(s - 1).wait_recv()
                own[s - 1] = raw[s - 1] + part_in[s - 1]

            to_core(s).start()

            @pl.when(s >= 1)
            def _():
                to_ring(s - 1).start()

            return carry

        lax.fori_loop(0, rings, step, 0)

        lane = iota((8, 128), 1)
        folded = tile_acc[:, :128] + tile_acc[:, 128:]
        folded = folded + pltpu.roll(folded, 64, 1)
        pix_in[p] = jnp.where(lane < 64, folded[:8], folded[8:])
        for k in range(1, pixs):
            to_all(*to_pix, k, pix_send, pix_recv).start()

        to_core(rings - 1).wait_recv()
        mine = raw[rings - 1] + part_in[rings - 1]

        for k in range(1, pixs):
            from_all(*to_pix, k, pix_send, pix_recv).wait_recv()
        total = pix_in[0]
        for k in range(1, pixs):
            total = total + pix_in[k]
        date_in[d] = total
        for k in range(1, dates):
            to_all(*to_date, k, date_send, date_recv).start()

        for s in range(rings - 1):
            to_ring(s).wait_recv()
        for off in range(1, rings):
            mine = mine + ici_in[off]
        level_in[d] = block_levels(mine, acc_prefix, acc_rows, acc_a, acc_sums)
        for k in range(1, dates):
            to_all(*to_level, k, level_send, level_recv).start()

        push_tile_tables(1)
        for k in range(1, dates):
            from_all(*to_date, k, date_send, date_recv).wait_recv()
        total = date_in[0]
        for k in range(1, dates):
            total = total + date_in[k]
        levels = tile_of(total, acc_ta, acc_tb, 1)
        row = iota((8, 128), 0)
        by_lane = jnp.where(lane == 0, levels[0], jnp.where(lane == 1, levels[1], levels[2]))
        by_row = jnp.where(row == 0, levels[0], jnp.where(row == 1, levels[1], levels[2]))
        tile_ref[...] = by_lane[:1]

        for k in range(1, dates):
            from_all(*to_level, k, level_send, level_recv).wait_recv()
        for v in range(4):
            wide = level_in[4 * v]
            for i in range(1, 4):
                wide = jnp.where(lane >= 32 * i, level_in[4 * v + i], wide)
            anomaly_ref[:, v * 128 : (v + 1) * 128] = (wide - by_row)[:3]

        for s in range(rings):
            to_core(s).wait_send()
        for s in range(rings - 1):
            to_ring(s).wait_send()
        for k in range(1, pixs):
            to_all(*to_pix, k, pix_send, pix_recv).wait_send()
        for k in range(1, dates):
            to_all(*to_date, k, date_send, date_recv).wait_send()
            to_all(*to_level, k, level_send, level_recv).wait_send()

    pl.run_scoped(
        body,
        pltpu.ACC(0)((128, 256), f32),
        pltpu.ACC(1)((128, 256), f32),
        pltpu.ACC(0)((128, 256), f32),
        pltpu.ACC(1)((128, 256), f32),
        pltpu.ACC(0)((64, 256), f32),
        pltpu.ACC(1)((64, 256), f32),
        pltpu.ACC(1)((48, 256), f32),
        pltpu.ACC(0)((16, 256), f32),
        pltpu.ACC(1)((16, 256), f32),
    )


def solution(mesh):
    dates, pixs = mesh.shape["date"], mesh.shape["pix"]
    rings = dates // 2

    def body(bin_index, clear_mask):
        frames, pixels = bin_index.shape
        blocks = pixels // BLOCK
        groups = blocks // dates // JOINED
        quarter = (rings, groups, UPPER, JOINED * LOWER)
        dma = pltpu.SemaphoreType.DMA
        anomaly, tile = pl.pallas_call(
            functools.partial(kernel, dates, pixs),
            out_shape=(
                jax.ShapeDtypeStruct((3, blocks), f32),
                jax.ShapeDtypeStruct((1, 128), f32),
            ),
            in_specs=[pl.BlockSpec(memory_space=pltpu.HBM)] * 2,
            out_specs=(pl.BlockSpec(memory_space=pltpu.VMEM),) * 2,
            scratch_shapes=[
                pltpu.VMEM((frames, pixels), jnp.int32),
                pltpu.VMEM((frames, pixels), bf16),
                *[pltpu.VMEM(quarter, f32) for _ in range(5)],
                pltpu.VMEM((UPPER, JOINED * LOWER), f32),
                pltpu.VMEM((pixs, 8, 128), f32),
                pltpu.VMEM((dates, 8, 128), f32),
                pltpu.VMEM((dates, 8, 128), f32),
                dma((2, rings)),
                dma((rings,)),
                dma((rings,)),
                dma((rings,)),
                dma((rings,)),
                dma((pixs,)),
                dma((pixs,)),
                dma((dates,)),
                dma((dates,)),
                dma((dates,)),
                dma((dates,)),
            ],
            compiler_params=pltpu.CompilerParams(collective_id=0, has_side_effects=True),
        )(bin_index, clear_mask)
        return anomaly, tile[0, :3]

    return jax.shard_map(
        body,
        mesh=mesh,
        in_specs=(P("date", "pix"), P("date", "pix")),
        out_specs=(P(None, "pix"), P()),
        check_vma=False,
    )
```

time: 137 us -> 36.7 us (0.27)
  blocking collectives: 88.7 us -> 0 us
  Pallas kernels: 0 us -> 33.4 us
  matrix products: 20.4 us -> 0 us
  local copies, waits for them, and re-layouts: 19 us -> 2.43 us
  other arithmetic: 5.54 us -> 0 us
  between operations: 2.68 us -> 0.64 us
    all_to_all x2 -> x0, blocking collectives: 55.7 us -> none  [the longest x1 38.2 us: summed_on_arrival(): lax.all_to_all(blocks, axis, split_axis=0, concat_axis=0, tiled=True)]
    pallas_call x0 -> x1, Pallas kernels: none -> 33.4 us  [body(): pl.pallas_call(functools.partial(kernel, dates, pixs), out_shape=(jax.Sha...]
    psum x4 -> x0, blocking collectives: 33 us -> none  [over_axes(): return functools.reduce(lax.psum, axes, x)]
    dot_general x2 -> x0, matrix products: 20.4 us -> none  [the longest x1 20.1 us: block_counts(): jnp.einsum('ghdp,gldp->ghl', upper_table, lower_table, preferred_element_...]
    another operation x3 -> x0, local copies, waits for them, and re-layouts: 5.41 us -> none  [the longest x2 5.29 us: cut_along(): x.reshape(*lengths[:dim], devices, lengths[dim] // devices, *lengths[dim...]
    select_n x2 -> x0, local copies, waits for them, and re-layouts: 4.86 us -> none  [the longest x1 2.43 us: block_counts(): lower_digit = chosen % 16]
    select_n x1 -> x0, other arithmetic: 3.84 us -> none  [block_counts(): upper_digit = chosen // 16]
    dot_general x1 -> x0, local copies, waits for them, and re-layouts: 3.23 us -> none  [block_counts(): jnp.einsum('ghdp,gldp->ghl', upper_table, lower_table, preferred_element_...]
where the time goes in v1:
time: 36.7 us; the launch traced here: 36.5 us
  Pallas kernels  33.4 us (91%)
  local copies, waits for them, and re-layouts  2.43 us (7%)
  between operations  0.64 us (2%)
    pallas_call x1, Pallas kernels, body(): pl.pallas_call(functools.partial(kernel, dates, pixs), out_shape=(jax.Sha...  33.4 us
    unnamed x1, local copies, waits for them, and re-layouts  1.3 us
    squeeze x1, local copies, waits for them, and re-layouts, body(): return (anomaly, tile[0, :3])  1.14 us

profile of v1, /device:TPU:1, one launch (start us, length us, event | category | flops | bytes accessed | tf_op | source)
XLA Modules:
  0.0 36.5 jit_solution(10893108305150510201)
XLA Ops:
  0.6 33.4 %shard_map.41 = (f32[3,512]{1,0:T(4,128)}, f32[1,128]{1,0:T(1,128)}) custom-call(s32[16,65536]{1,0:T(8,128)} %idx_hbm.1, bf16[16,65536]{1,0:T(8,128)(2,1)} %w_hbm.1), custom_call_target="tpu_custom_call" | custom-call | tf_op jit(solution)/shard_map/pallas_call | solution.py:389
  34.1 1.1 %slice_bitcast_fusion = f32[3]{0:T(128)} fusion(f32[1,128]{1,0:T(1,128)} %get-tuple-element.5), kind=kLoop, calls=%fused_computation | loop fusion | bytes 24 | tf_op jit(solution)/shard_map/squeeze | solution.py:419
  35.2 1.3 %copy.5 = f32[3,512]{1,0:T(4,128)} copy(f32[3,512]{1,0:T(4,128)} %get-tuple-element.8) | data formatting | bytes 12288

commit v2 on v1

--- a/solution.py
+++ b/solution.py
@@ -14,6 +14,10 @@
 JOINED = 8
 QUANTILES = (0.1, 0.5, 0.9)
 LOW_EDGE = -1.0
+AHEAD = (4, 2, 2, 3, 3, 1, 1, 0)
+HALF_AHEAD = (0, 0, 1, 0, 1, 0, 1, 0)
+HALF_BEHIND = (1, 0, 1, 0, 1, 0, 1, 1)
+FIRST_RELAYED = 3
 MESH = pl.DeviceIdType.MESH
 bf16 = jnp.bfloat16
 f32 = jnp.float32
@@ -36,7 +40,7 @@
     return first, second, third
 
 
-def count_group(idx_ref, w_ref, base, acc, mxu):
+def feed_group(idx_ref, w_ref, base, acc, mxu):
     upper_rows = (iota((UPPER, 128), 0) * LOWER).astype(jnp.int16)
     lower_rows = iota((LOWER, 128), 0).astype(jnp.int16)
     lefts, rights = [], []
@@ -62,6 +66,9 @@
         right = jnp.concatenate([jnp.concatenate([x[f] for f in pair], axis=1) for x in rights], axis=0)
         pltpu.matmul_push_rhs(right, staging_register=k % 2, mxu_index=mxu, transpose=True)
         pltpu.matmul_acc_lhs(acc, left, load_staged_rhs=k % 2)
+
+
+def drain_group(acc):
     joint = pltpu.matmul_pop(acc)
     lane = iota((UPPER, 128), 1)
     halves = []
@@ -172,6 +179,7 @@
     part_in,
     own,
     ici_in,
+    relay_in,
     tile_acc,
     pix_in,
     date_in,
@@ -181,6 +189,8 @@
     core_recv,
     ici_send,
     ici_recv,
+    relay_send,
+    relay_recv,
     pix_send,
     pix_recv,
     date_send,
@@ -195,24 +205,17 @@
     rings = dates // 2
     owner_lanes = idx_v.shape[1] // dates
     chunk = 2 * owner_lanes
-    half = rings // 2
-
-    def offset_of(s):
-        odd = lax.rem(s, 2)
-        return half + (1 - odd) * lax.div(s, 2) - odd * lax.div(s + 1, 2)
-
-    def ring_at(s):
-        return lax.rem(z + offset_of(s), rings)
-
-    def load(s):
-        lanes = pl.ds(pl.multiple_of(ring_at(s) * chunk, 128), chunk)
+
+    def load(off):
+        ring = lax.rem(z + off, rings)
+        lanes = pl.ds(pl.multiple_of(ring * chunk, 128), chunk)
         return (
-            pltpu.make_async_copy(idx_hbm.at[:, lanes], idx_v.at[:, lanes], in_sem.at[0, s]),
-            pltpu.make_async_copy(w_hbm.at[:, lanes], w_v.at[:, lanes], in_sem.at[1, s]),
-        )
-
-    for s in range(rings):
-        for copy in load(s):
+            pltpu.make_async_copy(idx_hbm.at[:, lanes], idx_v.at[:, lanes], in_sem.at[0, ring]),
+            pltpu.make_async_copy(w_hbm.at[:, lanes], w_v.at[:, lanes], in_sem.at[1, ring]),
+        )
+
+    for off in (4, 2, 6, 3, 5, 1, 7, 0):
+        for copy in load(off):
             copy.start()
 
     barrier = pltpu.get_barrier_semaphore()
@@ -225,116 +228,195 @@
         return pltpu.make_async_remote_copy(
             src_ref=part_out.at[s],
             dst_ref=part_in.at[s],
-            send_sem=core_send.at[s],
+            send_sem=core_send.at[0],
             recv_sem=core_recv.at[s],
             device_id={"date": d + 1 - 2 * core},
             device_id_type=MESH,
         )
 
-    def to_ring(s):
-        off = offset_of(s)
-        return pltpu.make_async_remote_copy(
-            src_ref=own.at[s],
-            dst_ref=ici_in.at[off],
-            send_sem=ici_send.at[s],
-            recv_sem=ici_recv.at[off],
+    def to_ring(s, off, side, half):
+        groups = pl.ds(2 * half, 2)
+        return pltpu.make_async_remote_copy(
+            src_ref=own.at[s, pl.ds(2 * side, 2)],
+            dst_ref=ici_in.at[off, groups],
+            send_sem=ici_send.at[0],
+            recv_sem=ici_recv.at[0],
             device_id={"date": 2 * lax.rem(z + off, rings) + core},
             device_id_type=MESH,
         )
 
-    def to_all(buffer, axis, me, size, k, send, recv):
+    def all_rings():
+        whole = own.at[pl.ds(0, rings - 2)]
+        return pltpu.make_async_remote_copy(
+            src_ref=whole,
+            dst_ref=ici_in.at[pl.ds(0, rings - 2)],
+            send_sem=ici_send.at[0],
+            recv_sem=ici_recv.at[0],
+            device_id={"date": d + 1 - 2 * core},
+            device_id_type=MESH,
+        )
+
+    def all_cores():
+        return pltpu.make_async_remote_copy(
+            src_ref=part_out,
+            dst_ref=part_in,
+            send_sem=core_send.at[0],
+            recv_sem=core_recv.at[0],
+            device_id={"date": d + 1 - 2 * core},
+            device_id_type=MESH,
+        )
+
+    def to_relay(side):
+        half = pl.ds(2 * side, 2)
+        return pltpu.make_async_remote_copy(
+            src_ref=own.at[0, half],
+            dst_ref=relay_in.at[side],
+            send_sem=relay_send.at[side],
+            recv_sem=relay_recv.at[side],
+            device_id={"date": 2 * lax.rem(z + (1 if side == 0 else rings - 1), rings) + core},
+            device_id_type=MESH,
+        )
+
+    def to_all(buffer, axis, me, size, send, recv, k):
         return pltpu.make_async_remote_copy(
             src_ref=buffer.at[me],
             dst_ref=buffer.at[me],
-            send_sem=send.at[k],
-            recv_sem=recv.at[me],
+            send_sem=send.at[0],
+            recv_sem=recv.at[0],
             device_id={axis: lax.rem(me + k, size)},
             device_id_type=MESH,
         )
 
-    def from_all(buffer, axis, me, size, k, send, recv):
-        source = lax.rem(me + k, size)
-        return pltpu.make_async_remote_copy(
-            src_ref=buffer.at[source],
-            dst_ref=buffer.at[source],
-            send_sem=send.at[k],
-            recv_sem=recv.at[source],
-            device_id={axis: source},
-            device_id_type=MESH,
-        )
-
-    to_pix = (pix_in, "pix", p, pixs)
-    to_date = (date_in, "date", d, dates)
-    to_level = (level_in, "date", d, dates)
+    def whole_of(buffer, axis, me, size, send, recv):
+        others = buffer.at[pl.ds(0, size - 1)]
+        return pltpu.make_async_remote_copy(
+            src_ref=others,
+            dst_ref=others,
+            send_sem=send.at[0],
+            recv_sem=recv.at[0],
+            device_id={axis: lax.rem(me + 1, size)},
+            device_id_type=MESH,
+        )
+
+    to_pix = (pix_in, "pix", p, pixs, pix_send, pix_recv)
+    to_date = (date_in, "date", d, dates, date_send, date_recv)
+    to_level = (level_in, "date", d, dates, level_send, level_recv)
 
     def body(acc_a, acc_b, acc_c, acc_d, acc_prefix, acc_rows, acc_sums, acc_ta, acc_tb):
         tile_acc[...] = jnp.zeros_like(tile_acc)
 
+        accs = (acc_a, acc_b, acc_c, acc_d)
+
         def step(s, carry):
-            for copy in load(s):
-                copy.wait()
-            ring = ring_at(s)
+            codes, last = carry
+            ahead, half_a, half_b = lax.rem(codes[0], rings), lax.rem(codes[1], 2), lax.rem(codes[2], 2)
+            behind = lax.rem(rings - ahead, rings)
+
+            @pl.when((s == 0) | (half_a == 0))
+            def _():
+                for copy in load(ahead):
+                    copy.wait()
+
+            @pl.when((s > 0) & (s < rings - 1) & (half_a == 0))
+            def _():
+                for copy in load(behind):
+                    copy.wait()
+
+            ring_a, ring_b = lax.rem(z + ahead, rings), lax.rem(z + behind, rings)
+
+            def base_of(m):
+                side = 1 - core if m < 4 else core
+                ring, half = (ring_a, half_a) if m % 4 < 2 else (ring_b, half_b)
+                return (2 * ring + side) * owner_lanes + (2 * half + m % 2) * (JOINED * BLOCK)
+
             sums = None
             for m in range(8):
-                side = 1 - core if m < 4 else core
-                base = (2 * ring + side) * owner_lanes + (m % 4) * (JOINED * BLOCK)
-                counts = count_group(idx_v, w_v, base, (acc_a, acc_b, acc_c, acc_d)[m % 4], m % 2)
-                if m < 4:
-                    part_out[s, m] = counts
-                else:
-                    raw[s, m - 4] = counts
-                sums = counts if sums is None else sums + counts
+                feed_group(idx_v, w_v, base_of(m), accs[m % 4], m % 2)
+                if m < 6:
+                    counts = drain_group(accs[m % 4])
+                    if m < 4:
+                        part_out[s, m] = counts
+                    else:
+                        raw[s, m - 4] = counts
+                    sums = counts if sums is None else sums + counts
             tile_acc[...] += sums
 
             @pl.when(s == 0)
             def _():
                 pl.semaphore_wait(barrier, dates + pixs - 2)
+
+            to_core(s).start()
 
             @pl.when(s >= 1)
             def _():
                 to_core(s - 1).wait_recv()
                 own[s - 1] = raw[s - 1] + part_in[s - 1]
 
-            to_core(s).start()
-
-            @pl.when(s >= 1)
+            @pl.when(s == 1)
             def _():
-                to_ring(s - 1).start()
-
-            return carry
-
-        lax.fori_loop(0, rings, step, 0)
+                to_relay(0).start()
+                to_relay(1).start()
+
+            for side in range(2):
+                at = FIRST_RELAYED + side
+
+                @pl.when(s == at + 1)
+                def _(side=side, at=at):
+                    to_relay(side).wait_recv()
+                    own[at, 2 * side : 2 * side + 2] += relay_in[side]
+
+            @pl.when(s >= 2)
+            def _():
+                to_ring(s - 1, last[0], 0, last[1]).start()
+                to_ring(s - 1, rings - last[0], 1, last[1]).start()
+
+            for m in (6, 7):
+                counts = drain_group(accs[m % 4])
+                raw[s, m - 4] = counts
+                tile_acc[...] += counts
+            return (lax.div(codes[0], rings), lax.div(codes[1], 2), lax.div(codes[2], 2)), (ahead, half_a)
+
+        codes = (
+            jnp.int32(sum(v * rings**s for s, v in enumerate(AHEAD))),
+            jnp.int32(sum(v * 2**s for s, v in enumerate(HALF_AHEAD))),
+            jnp.int32(sum(v * 2**s for s, v in enumerate(HALF_BEHIND))),
+        )
+        lax.fori_loop(0, rings, step, (codes, (jnp.int32(0), jnp.int32(0))))
 
         lane = iota((8, 128), 1)
         folded = tile_acc[:, :128] + tile_acc[:, 128:]
         folded = folded + pltpu.roll(folded, 64, 1)
         pix_in[p] = jnp.where(lane < 64, folded[:8], folded[8:])
         for k in range(1, pixs):
-            to_all(*to_pix, k, pix_send, pix_recv).start()
+            to_all(*to_pix, k).start()
+        push_tile_tables(1)
 
         to_core(rings - 1).wait_recv()
         mine = raw[rings - 1] + part_in[rings - 1]
 
-        for k in range(1, pixs):
-            from_all(*to_pix, k, pix_send, pix_recv).wait_recv()
+        all_rings().wait_recv()
+        for off in range(1, rings):
+            if off != rings // 2:
+                mine = mine + ici_in[off]
+        level_in[d] = block_levels(mine, acc_prefix, acc_rows, acc_a, acc_sums)
+        for k in range(1, dates):
+            to_all(*to_level, k).start()
+
+        whole_of(*to_pix).wait_recv()
         total = pix_in[0]
         for k in range(1, pixs):
             total = total + pix_in[k]
         date_in[d] = total
         for k in range(1, dates):
-            to_all(*to_date, k, date_send, date_recv).start()
-
-        for s in range(rings - 1):
-            to_ring(s).wait_recv()
-        for off in range(1, rings):
-            mine = mine + ici_in[off]
-        level_in[d] = block_levels(mine, acc_prefix, acc_rows, acc_a, acc_sums)
-        for k in range(1, dates):
-            to_all(*to_level, k, level_send, level_recv).start()
-
-        push_tile_tables(1)
-        for k in range(1, dates):
-            from_all(*to_date, k, date_send, date_recv).wait_recv()
+            to_all(*to_date, k).start()
+
+        all_cores().wait_send()
+        for side in range(2):
+            to_relay(side).wait_send()
+        all_rings().wait_send()
+        whole_of(*to_pix).wait_send()
+
+        whole_of(*to_date).wait_recv()
         total = date_in[0]
         for k in range(1, dates):
             total = total + date_in[k]
@@ -344,23 +426,15 @@
         by_row = jnp.where(row == 0, levels[0], jnp.where(row == 1, levels[1], levels[2]))
         tile_ref[...] = by_lane[:1]
 
-        for k in range(1, dates):
-            from_all(*to_level, k, level_send, level_recv).wait_recv()
+        whole_of(*to_level).wait_recv()
         for v in range(4):
             wide = level_in[4 * v]
             for i in range(1, 4):
                 wide = jnp.where(lane >= 32 * i, level_in[4 * v + i], wide)
             anomaly_ref[:, v * 128 : (v + 1) * 128] = (wide - by_row)[:3]
 
-        for s in range(rings):
-            to_core(s).wait_send()
-        for s in range(rings - 1):
-            to_ring(s).wait_send()
-        for k in range(1, pixs):
-            to_all(*to_pix, k, pix_send, pix_recv).wait_send()
-        for k in range(1, dates):
-            to_all(*to_date, k, date_send, date_recv).wait_send()
-            to_all(*to_level, k, level_send, level_recv).wait_send()
+        whole_of(*to_date).wait_send()
+        whole_of(*to_level).wait_send()
 
     pl.run_scoped(
         body,
@@ -376,9 +450,15 @@
     )
 
 
+def finish(anomaly_ref, tile_ref, anomaly_out, tile_out):
+    anomaly_out[...] = anomaly_ref[...]
+    tile_out[...] = tile_ref[0, :3]
+
+
 def solution(mesh):
     dates, pixs = mesh.shape["date"], mesh.shape["pix"]
     rings = dates // 2
+    assert rings == len(AHEAD)
 
     def body(bin_index, clear_mask):
         frames, pixels = bin_index.shape
@@ -398,25 +478,34 @@
                 pltpu.VMEM((frames, pixels), jnp.int32),
                 pltpu.VMEM((frames, pixels), bf16),
                 *[pltpu.VMEM(quarter, f32) for _ in range(5)],
+                pltpu.VMEM((2, 2, UPPER, JOINED * LOWER), f32),
                 pltpu.VMEM((UPPER, JOINED * LOWER), f32),
                 pltpu.VMEM((pixs, 8, 128), f32),
                 pltpu.VMEM((dates, 8, 128), f32),
                 pltpu.VMEM((dates, 8, 128), f32),
                 dma((2, rings)),
+                dma((1,)),
                 dma((rings,)),
-                dma((rings,)),
-                dma((rings,)),
-                dma((rings,)),
-                dma((pixs,)),
-                dma((pixs,)),
-                dma((dates,)),
-                dma((dates,)),
-                dma((dates,)),
-                dma((dates,)),
+                dma((1,)),
+                dma((1,)),
+                dma((2,)),
+                dma((2,)),
+                *[dma((1,)) for _ in range(6)],
             ],
-            compiler_params=pltpu.CompilerParams(collective_id=0, has_side_effects=True),
+            compiler_params=pltpu.CompilerParams(
+                collective_id=0, has_side_effects=True, vmem_limit_bytes=52 * 1024 * 1024
+            ),
         )(bin_index, clear_mask)
-        return anomaly, tile[0, :3]
+        return pl.pallas_call(
+            finish,
+            out_shape=(
+                jax.ShapeDtypeStruct((3, blocks), f32),
+                jax.ShapeDtypeStruct((3,), f32),
+            ),
+            in_specs=[pl.BlockSpec(memory_space=pltpu.VMEM)] * 2,
+            out_specs=(pl.BlockSpec(memory_space=pltpu.VMEM),) * 2,
+            compiler_params=pltpu.CompilerParams(vmem_limit_bytes=1024 * 1024),
+        )(anomaly, tile)
 
     return jax.shard_map(
         body,

time: 36.7 us -> 32.9 us (0.90)
  local copies, waits for them, and re-layouts: 2.43 us -> 0 us
  Pallas kernels: 33.4 us -> 32.2 us
    pallas_call x1, Pallas kernels: 33.4 us -> 31.6 us  [body(): pl.pallas_call(functools.partial(kernel, dates, pixs), out_shape=(jax.Sha...]
    unnamed x1 -> x0, local copies, waits for them, and re-layouts: 1.3 us -> none
    squeeze x1 -> x0, local copies, waits for them, and re-layouts: 1.14 us -> none  [body(): return (anomaly, tile[0, :3])]
    pallas_call x0 -> x1, Pallas kernels: none -> 0.6 us  [body(): pl.pallas_call(finish, out_shape=(jax.ShapeDtypeStruct((3, blocks), f32),...]
where the time goes in v2:
time: 32.9 us; the launch traced here: 32.8 us
  Pallas kernels  32.2 us (98%)
  between operations  0.64 us (2%)
    pallas_call x1, Pallas kernels, body(): pl.pallas_call(functools.partial(kernel, dates, pixs), out_shape=(jax.Sha...  31.6 us

profile of v2, /device:TPU:1, one launch (start us, length us, event | category | flops | bytes accessed | tf_op | source)
XLA Modules:
  0.0 32.8 jit_solution(986816665901315576)
XLA Ops:
  0.6 31.6 %shard_map.41 = (f32[3,512]{1,0:T(4,128)S(1)}, f32[1,128]{1,0:T(1,128)S(1)}) custom-call(s32[16,65536]{1,0:T(8,128)} %idx_hbm.1, bf16[16,65536]{1,0:T(8,128)(2,1)} %w_hbm.1), custom_call_target="tpu_custom_call" | custom-call | tf_op jit(solution)/shard_map/pallas_call | solution.py:469
  32.2 0.6 %shard_map.42 = (f32[3,512]{1,0:T(4,128)}, f32[3]{0:T(128)}) custom-call(f32[3,512]{1,0:T(4,128)S(1)} %get-tuple-element.4.anomaly_ref, f32[1,128]{1,0:T(1,128)S(1)} %get-tuple-element.5.tile_ref), custom_call_target="tpu_custom_call" | custom-call | tf_op jit(solution)/shard_map/pallas_call | solution.py:499

commit v3 on v2

--- a/solution.py
+++ b/solution.py
@@ -87,20 +87,27 @@
         pltpu.matmul_acc_lhs(acc, piece, load_staged_rhs=register if n == 0 else None)
 
 
-def block_levels(counts, acc_prefix, acc_rows, acc_below, acc_sums):
-    flat = counts.reshape(64, 256)
+def build_level_tables(chosen_ref, sums_ref):
     r, c = iota((256, 256), 0), iota((256, 256), 1)
     same = (r // LOWER) == (c // LOWER)
     pltpu.matmul_push_rhs(ones_where(same & (r % LOWER < c % LOWER)), staging_register=0, mxu_index=0)
     pltpu.matmul_push_rhs(ones_where(same), staging_register=0, mxu_index=1)
+    i, k = iota((128, 256), 0), iota((128, 256), 1)
+    chosen_ref[...] = ones_where(
+        ((i % 64) // UPPER == (k % 64) // UPPER) & (k < 192) & ((k % UPPER < i % UPPER) | (i >= 64))
+    )
+    for g in range(4):
+        sums_ref[g] = ones_where((c % LOWER) == JOINED * g + r // LOWER)
+
+
+def block_levels(counts, chosen_ref, sums_ref, acc_prefix, acc_rows, acc_below, acc_sums):
+    flat = counts.reshape(64, 256)
+    triple_matmul(acc_rows, flat, 0)
     triple_matmul(acc_prefix, flat, 0)
-    triple_matmul(acc_rows, flat, 0)
     row_sums = pltpu.matmul_pop(acc_rows)
     stacked = jnp.concatenate([*pieces(row_sums), jnp.zeros((64, 256), bf16)], axis=0)
     pltpu.matmul_push_rhs(stacked, staging_register=0, mxu_index=0)
-    i, k = iota((128, 256), 0), iota((128, 256), 1)
-    chosen = ((i % 64) // UPPER == (k % 64) // UPPER) & (k < 192) & ((k % UPPER < i % UPPER) | (i >= 64))
-    pltpu.matmul_acc_lhs(acc_below, ones_where(chosen), load_staged_rhs=0)
+    pltpu.matmul_acc_lhs(acc_below, chosen_ref[...], load_staged_rhs=0)
     within = pltpu.matmul_pop(acc_prefix)
     below = pltpu.matmul_pop(acc_below)
     before = within + below[:64]
@@ -108,14 +115,12 @@
     floor = jnp.maximum(flat, 1.0)
     passed = [jnp.clip((q * total + 0.25 - before) / floor, 0.0, 1.0) for q in QUANTILES]
     for g in range(4):
-        pltpu.matmul_push_rhs(
-            ones_where((c % LOWER) == JOINED * g + r // LOWER), staging_register=0, mxu_index=1
-        )
+        pltpu.matmul_push_rhs(sums_ref[g], staging_register=0, mxu_index=1)
         rows = jnp.concatenate([p[g * UPPER : (g + 1) * UPPER] for p in passed], axis=0)
         triple_matmul(acc_sums, rows, 0)
     sums = pltpu.matmul_pop(acc_sums)[:, :128]
-    row = iota((8, 128), 0)
-    out = jnp.zeros((8, 128), f32)
+    row = iota((4, 128), 0)
+    out = jnp.zeros((4, 128), f32)
     for q in range(3):
         value = jnp.sum(sums[q * UPPER : (q + 1) * UPPER], axis=0, keepdims=True)
         out = jnp.where(row == q, LOW_EDGE + 2.0 / BINS * value, out)
@@ -124,15 +129,18 @@
 
 def push_tile_tables(register):
     r, c = iota((256, 256), 0), iota((256, 256), 1)
-    same = (r % 128) // 64 == (c % 128) // 64
-    counts = same & (r % LOWER == c % LOWER) & (c < 128)
-    prefix = same & (r % LOWER < c % LOWER) & (c >= 128)
-    pltpu.matmul_push_rhs(ones_where(counts | prefix), staging_register=register, mxu_index=0)
-    pltpu.matmul_push_rhs(ones_where(same | (c >= 128)), staging_register=register, mxu_index=1)
+    r_part, c_part = (r % 128) // LOWER, (c % 128) // LOWER
+    same = r_part == c_part
+    prefix = same & (r % LOWER < c % LOWER)
+    pltpu.matmul_push_rhs(ones_where((c >= 128) | prefix), staging_register=register, mxu_index=0)
+    pltpu.matmul_push_rhs(
+        ones_where(((c < 128) & same) | ((c >= 128) & (r_part < c_part))), staging_register=register, mxu_index=1
+    )
 
 
 def tile_of(total, acc_a, acc_b, register):
-    p1, p2, p3 = pieces(total)
+    counts = jnp.concatenate([total, jnp.zeros((4, 128), f32)], axis=0)
+    p1, p2, p3 = pieces(counts)
     zero = jnp.zeros((8, 128), f32)
     left = jnp.concatenate(
         [
@@ -147,21 +155,23 @@
     b = pltpu.matmul_pop(acc_b)
     a = a[:8] + a[8:]
     b = b[:8] + b[8:]
-    counts, within = a[:, :128], a[:, 128:]
-    same_rows, all_rows = b[:, :128], b[:, 128:]
-    row, lane = iota((8, 128), 0), iota((8, 128), 1)
+    within, all_rows = a[:, :128], a[:, 128:]
+    same_rows, parts_below = b[:, :128], b[:, 128:]
+    row = iota((8, 128), 0)
     below = jnp.where(row >= 1, pltpu.roll(same_rows, 1, 0), 0.0)
+    for shift in (1, 2):
+        below = below + jnp.where(row >= shift, pltpu.roll(below, shift, 0), 0.0)
     for shift in (1, 2, 4):
-        below = below + jnp.where(row >= shift, pltpu.roll(below, shift, 0), 0.0)
-        same_rows = same_rows + pltpu.roll(same_rows, shift, 0)
         all_rows = all_rows + pltpu.roll(all_rows, shift, 0)
-    before = within + below + jnp.where(lane >= 64, all_rows - same_rows, 0.0)
+        parts_below = parts_below + pltpu.roll(parts_below, shift, 0)
+    before = within + below + parts_below
     floor = jnp.maximum(counts, 1.0)
     levels = []
     for q in QUANTILES:
         passed = jnp.clip((q * all_rows + 0.25 - before) / floor, 0.0, 1.0)
-        both = jnp.sum(jnp.sum(passed, axis=0, keepdims=True), axis=1, keepdims=True)
-        levels.append(LOW_EDGE + 2.0 / BINS * (0.5 * both))
+        passed = jnp.where(row < 4, passed, 0.0)
+        passed = jnp.sum(jnp.sum(passed, axis=0, keepdims=True), axis=1, keepdims=True)
+        levels.append(LOW_EDGE + 2.0 / BINS * passed)
     return levels
 
 
@@ -181,6 +191,8 @@
     ici_in,
     relay_in,
     tile_acc,
+    chosen_ref,
+    sums_ref,
     pix_in,
     date_in,
     level_in,
@@ -214,15 +226,17 @@
             pltpu.make_async_copy(w_hbm.at[:, lanes], w_v.at[:, lanes], in_sem.at[1, ring]),
         )
 
-    for off in (4, 2, 6, 3, 5, 1, 7, 0):
-        for copy in load(off):
-            copy.start()
-
+    for copy in load(AHEAD[0]):
+        copy.start()
     barrier = pltpu.get_barrier_semaphore()
     for k in range(1, dates):
         pl.semaphore_signal(barrier, inc=1, device_id={"date": lax.rem(d + k, dates)}, device_id_type=MESH)
     for k in range(1, pixs):
         pl.semaphore_signal(barrier, inc=1, device_id={"pix": lax.rem(p + k, pixs)}, device_id_type=MESH)
+
+    for off in (2, 6, 3, 5, 1, 7, 0):
+        for copy in load(off):
+            copy.start()
 
     def to_core(s):
         return pltpu.make_async_remote_copy(
@@ -383,24 +397,21 @@
         )
         lax.fori_loop(0, rings, step, (codes, (jnp.int32(0), jnp.int32(0))))
 
-        lane = iota((8, 128), 1)
         folded = tile_acc[:, :128] + tile_acc[:, 128:]
         folded = folded + pltpu.roll(folded, 64, 1)
-        pix_in[p] = jnp.where(lane < 64, folded[:8], folded[8:])
+        folded = folded + pltpu.roll(folded, 32, 1)
+        lane = iota((4, 128), 1)
+        packed = folded[:4]
+        for i in range(1, 4):
+            packed = jnp.where(lane >= 32 * i, folded[4 * i : 4 * i + 4], packed)
+        pix_in[p] = packed
         for k in range(1, pixs):
             to_all(*to_pix, k).start()
         push_tile_tables(1)
+        build_level_tables(chosen_ref, sums_ref)
 
         to_core(rings - 1).wait_recv()
-        mine = raw[rings - 1] + part_in[rings - 1]
-
-        all_rings().wait_recv()
-        for off in range(1, rings):
-            if off != rings // 2:
-                mine = mine + ici_in[off]
-        level_in[d] = block_levels(mine, acc_prefix, acc_rows, acc_a, acc_sums)
-        for k in range(1, dates):
-            to_all(*to_level, k).start()
+        raw[rings - 1] += part_in[rings - 1]
 
         whole_of(*to_pix).wait_recv()
         total = pix_in[0]
@@ -410,6 +421,15 @@
         for k in range(1, dates):
             to_all(*to_date, k).start()
 
+        all_rings().wait_recv()
+        mine = raw[rings - 1]
+        for off in range(1, rings):
+            if off != rings // 2:
+                mine = mine + ici_in[off]
+        level_in[d] = block_levels(mine, chosen_ref, sums_ref, acc_prefix, acc_rows, acc_a, acc_sums)
+        for k in range(1, dates):
+            to_all(*to_level, k).start()
+
         all_cores().wait_send()
         for side in range(2):
             to_relay(side).wait_send()
@@ -421,7 +441,7 @@
         for k in range(1, dates):
             total = total + date_in[k]
         levels = tile_of(total, acc_ta, acc_tb, 1)
-        row = iota((8, 128), 0)
+        row = iota((4, 128), 0)
         by_lane = jnp.where(lane == 0, levels[0], jnp.where(lane == 1, levels[1], levels[2]))
         by_row = jnp.where(row == 0, levels[0], jnp.where(row == 1, levels[1], levels[2]))
         tile_ref[...] = by_lane[:1]
@@ -480,9 +500,11 @@
                 *[pltpu.VMEM(quarter, f32) for _ in range(5)],
                 pltpu.VMEM((2, 2, UPPER, JOINED * LOWER), f32),
                 pltpu.VMEM((UPPER, JOINED * LOWER), f32),
-                pltpu.VMEM((pixs, 8, 128), f32),
-                pltpu.VMEM((dates, 8, 128), f32),
-                pltpu.VMEM((dates, 8, 128), f32),
+                pltpu.VMEM((128, 256), bf16),
+                pltpu.VMEM((4, 256, 256), bf16),
+                pltpu.VMEM((pixs, 4, 128), f32),
+                pltpu.VMEM((dates, 4, 128), f32),
+                pltpu.VMEM((dates, 4, 128), f32),
                 dma((2, rings)),
                 dma((1,)),
                 dma((rings,)),

time: 32.9 us -> 32.3 us (0.982)
  Pallas kernels: 32.2 us -> 31.5 us
    pallas_call x1, Pallas kernels: 31.6 us -> 30.9 us  [body(): pl.pallas_call(functools.partial(kernel, dates, pixs), out_shape=(jax.Sha...]
where the time goes in v3:
time: 32.3 us; the launch traced here: 32.2 us
  Pallas kernels  31.5 us (98%)
  between operations  0.64 us (2%)
    pallas_call x1, Pallas kernels, body(): pl.pallas_call(functools.partial(kernel, dates, pixs), out_shape=(jax.Sha...  30.9 us

profile of v3, /device:TPU:1, one launch (start us, length us, event | category | flops | bytes accessed | tf_op | source)
XLA Modules:
  0.0 32.2 jit_solution(9785636648220148501)
XLA Ops:
  0.6 30.9 %shard_map.41 = (f32[3,512]{1,0:T(4,128)S(1)}, f32[1,128]{1,0:T(1,128)S(1)}) custom-call(s32[16,65536]{1,0:T(8,128)} %idx_hbm.1, bf16[16,65536]{1,0:T(8,128)(2,1)} %w_hbm.1), custom_call_target="tpu_custom_call" | custom-call | tf_op jit(solution)/shard_map/pallas_call | solution.py:489
  31.6 0.6 %shard_map.42 = (f32[3,512]{1,0:T(4,128)}, f32[3]{0:T(128)}) custom-call(f32[3,512]{1,0:T(4,128)S(1)} %get-tuple-element.4.anomaly_ref, f32[1,128]{1,0:T(1,128)S(1)} %get-tuple-element.5.tile_ref), custom_call_target="tpu_custom_call" | custom-call | tf_op jit(solution)/shard_map/pallas_call | solution.py:521
